TPU v7x, 32 devices: a whole 2x2x4 slice. The times are simulated.
32 devices in a mesh: seq: 16 (over z, x, core), chan: 2 (over y).
Axes of the slice: x: 2, y: 2, z: 4, core: 2. Of those that a mesh axis runs over, the one named last changes fastest.
Arguments:
- step_size: bfloat16 [2, 5120, 2048], P(None, ('chan', 'seq')), as said below
- inputs: bfloat16 [2, 5120, 2048], P(None, ('chan', 'seq')), may hold values from -6 to 6
- gate_input: bfloat16 [2, 5120, 2048], P(None, ('chan', 'seq')), may hold values from -6 to 6
- decay_rate: float32 [5120], P('chan'), as said below
- norm_gain: float32 [5120], P('chan'), may hold values from 0.1 to 1.9
- resets: int32 [2, 8], replicated, may hold values from 1 to 2047
Outputs:
- normed: bfloat16 [2, 5120, 2048], P(None, 'chan', 'seq')
Inputs may be any that keep to these rules, and one draw needn't show every extreme that they name: `step_size`: positive step sizes. `decay_rate`: positive rates. `resets`: positions within the sequence; several may coincide.
All inputs are finite; a program needn't handle non-finite values.
Results may differ from a plain program's by a relative error of at most 0.001.
Values may be sent and summed in bfloat16 or wider, within the bound.
A program may use at most 64 MiB of HBM per device.

v0:
```python
import math

import jax
import jax.numpy as jnp
from jax import lax
from jax.sharding import PartitionSpec as P

FEATURE_WIDTH = 5120


def compose(earlier, later):
    return (earlier[0] * later[0], later[0] * earlier[1] + later[1])


def coefficients(steps, values, rates):
    scaled = steps.astype(jnp.float32) * rates[None, :, None]
    drive = jnp.sqrt(-jnp.expm1(-2.0 * scaled)) * values.astype(jnp.float32)
    return (scaled, drive)


def marks_for(resets, places):
    return jnp.any(resets[:, :, None] == places[None, None, :], axis=1)


def local_scan(scaled, drive, marks):
    rows, chans, length = scaled.shape
    places = jnp.arange(length, dtype=jnp.int32)
    upper = (places[:, None] <= places[None, :]).astype(jnp.float32)
    cumul = jnp.einsum("rck,ku->rcu", scaled, upper, precision=lax.Precision.HIGHEST)
    counts = jnp.dot(marks.astype(jnp.float32), upper, precision=lax.Precision.HIGHEST)
    linked = (counts[:, :, None] == counts[:, None, :]) & (places[:, None] >= places[None, :])[None]
    group = math.gcd(chans, 64)

    def one_group(pieces):
        cumul_part, drive_part = pieces
        spread = cumul_part[:, :, :, None] - cumul_part[:, :, None, :]
        weight = jnp.where(linked[:, None], jnp.exp(-jnp.maximum(spread, 0.0)), jnp.float32(0.0))
        return jnp.einsum("rctj,rcj->rct", weight, drive_part, precision=lax.Precision.HIGHEST)

    def split_groups(array):
        return jnp.moveaxis(array.reshape(rows, chans // group, group, length), 1, 0)

    results = lax.map(one_group, (split_groups(cumul), split_groups(drive)))
    local_state = jnp.moveaxis(results, 0, 1).reshape(rows, chans, length)
    running = jnp.where(counts[:, None, :] == 0.0, jnp.exp(-cumul), jnp.float32(0.0))
    return (running, local_state)


def finish(gated, norm_gain):
    squares = jnp.sum(gated * gated, axis=1)
    total = lax.psum(squares, "chan")
    mean_square = total / jnp.float32(FEATURE_WIDTH)
    scale_rows = lax.rsqrt(mean_square + 1e-05)
    return (gated * scale_rows[:, None, :] * norm_gain[None, :, None]).astype(jnp.bfloat16)


def per_device(step_size, inputs, gate_input, decay_rate, norm_gain, resets):
    position = lax.axis_index("seq")
    batch, width, length = step_size.shape
    rates = lax.dynamic_slice_in_dim(decay_rate, position * width, width)
    places = jnp.arange(length, dtype=jnp.int32)
    scaled, drive = coefficients(step_size, inputs, rates)
    marks = marks_for(resets, places)
    piece = math.gcd(length, 128)
    count_blocks = length // piece

    def to_blocks(array):
        moved = jnp.moveaxis(array.reshape(batch, width, count_blocks, piece), 2, 1)
        return moved.reshape(batch * count_blocks, width, piece)

    running, local_state = local_scan(
        to_blocks(scaled), to_blocks(drive), marks.reshape(batch * count_blocks, piece)
    )
    total_decay = running[:, :, -1].reshape(batch, count_blocks, width)
    total_state = local_state[:, :, -1].reshape(batch, count_blocks, width)
    prefix = lax.associative_scan(compose, (total_decay, total_state), axis=1)
    incoming = jnp.concatenate(
        [jnp.zeros((batch, 1, width), jnp.float32), prefix[1][:, :-1]], axis=1
    )
    blocked = local_state + running * incoming.reshape(batch * count_blocks, width)[:, :, None]
    state = jnp.moveaxis(blocked.reshape(batch, count_blocks, width, piece), 1, 2).reshape(
        batch, width, length
    )
    local_gated = state * jax.nn.silu(gate_input.astype(jnp.float32))
    gated = lax.all_to_all(local_gated, "seq", split_axis=2, concat_axis=1, tiled=True)
    return finish(gated, norm_gain)


def solution(mesh):
    in_specs = (
        P(None, ("chan", "seq"), None),
        P(None, ("chan", "seq"), None),
        P(None, ("chan", "seq"), None),
        P("chan"),
        P("chan"),
        P(),
    )
    out_specs = P(None, "chan", "seq")
    return jax.shard_map(
        per_device, mesh=mesh, in_specs=in_specs, out_specs=out_specs, check_vma=False
    )
```

profile of v0, /device:TPU:0, one launch (start us, length us, event | category | flops | bytes accessed | tf_op | source)
XLA Modules:
  0.0 738.9 jit_solution(2449741942070967262)
XLA Ops:
  0.8 5.1 convert_multiply_fusion.1
  7.7 2.9 exponential_select_fusion
  10.8 1.5 copy-done.2
  13.0 2.3 copy.53
  15.3 581.5 %while.11 = (s32[]{:T(128)}, f32[5,32,32,128]{3,2,1,0:T(8,128)}, f32[5,32,32,128]{3,2,1,0:T(8,128)S(1)}, f32[5,32,32,128]{3,2,0,1:T(8,128)}, f32[32,128]{1,0:T(8...) while((s32[]{:T(128)}, f32[5,32,32,128]{3,2,1,0:T(8,128)}, f32[5,32,32,128]{3,2,1,0:T(8,128)S(1)}, ...), condition=%wide.region_2.3_spmd.clone, body=%wide.region_1.2_spmd.clone.sunk | while | flops 269484032 | bytes 5800533 | solution.py:43
  29.8 1.1 constant_dynamic-slice_fusion.2
  31.6 110.7 %fusion.44 = f32[32,32,1,128]{3,2,1,0:T(1,128)S(1)} fusion(f32[32,32,128,1]{2,3,1,0:T(1,128)S(1)} %bitcast.83, f32[32,32,128]{2,1,0:T(8,128)S(1)} %dynamic-slice_bitcast_fusion.2, pred[32,128,128]{2,1,0:T(8,128)(4,1)S(1)} %compare_and_fusion.2), kind=kOutput, calls=%fused_computation.1.clone.2 | convolution fusion | flops 268435456 | bytes 2097152 | tf_op jit(solution)/shard_map/while/body/eval_jaxpr/rctj,rcj->rct/dot_general | solution.py:38
  143.2 1.1 constant_dynamic-slice_fusion.2
  145.0 110.7 %fusion.44 = f32[32,32,1,128]{3,2,1,0:T(1,128)S(1)} fusion(f32[32,32,128,1]{2,3,1,0:T(1,128)S(1)} %bitcast.83, f32[32,32,128]{2,1,0:T(8,128)S(1)} %dynamic-slice_bitcast_fusion.2, pred[32,128,128]{2,1,0:T(8,128)(4,1)S(1)} %compare_and_fusion.2), kind=kOutput, calls=%fused_computation.1.clone.2 | convolution fusion | flops 268435456 | bytes 2097152 | tf_op jit(solution)/shard_map/while/body/eval_jaxpr/rctj,rcj->rct/dot_general | solution.py:38
  255.7 0.9 constant_dynamic-update-slice_fusion.2
  256.6 1.1 constant_dynamic-slice_fusion.2
  258.5 110.7 %fusion.44 = f32[32,32,1,128]{3,2,1,0:T(1,128)S(1)} fusion(f32[32,32,128,1]{2,3,1,0:T(1,128)S(1)} %bitcast.83, f32[32,32,128]{2,1,0:T(8,128)S(1)} %dynamic-slice_bitcast_fusion.2, pred[32,128,128]{2,1,0:T(8,128)(4,1)S(1)} %compare_and_fusion.2), kind=kOutput, calls=%fused_computation.1.clone.2 | convolution fusion | flops 268435456 | bytes 2097152 | tf_op jit(solution)/shard_map/while/body/eval_jaxpr/rctj,rcj->rct/dot_general | solution.py:38
  369.2 0.9 constant_dynamic-update-slice_fusion.2
  370.0 1.1 constant_dynamic-slice_fusion.2
  371.9 110.7 %fusion.44 = f32[32,32,1,128]{3,2,1,0:T(1,128)S(1)} fusion(f32[32,32,128,1]{2,3,1,0:T(1,128)S(1)} %bitcast.83, f32[32,32,128]{2,1,0:T(8,128)S(1)} %dynamic-slice_bitcast_fusion.2, pred[32,128,128]{2,1,0:T(8,128)(4,1)S(1)} %compare_and_fusion.2), kind=kOutput, calls=%fused_computation.1.clone.2 | convolution fusion | flops 268435456 | bytes 2097152 | tf_op jit(solution)/shard_map/while/body/eval_jaxpr/rctj,rcj->rct/dot_general | solution.py:38
  482.6 0.9 constant_dynamic-update-slice_fusion.2
  483.4 1.1 constant_dynamic-slice_fusion.2
  485.3 110.7 %fusion.44 = f32[32,32,1,128]{3,2,1,0:T(1,128)S(1)} fusion(f32[32,32,128,1]{2,3,1,0:T(1,128)S(1)} %bitcast.83, f32[32,32,128]{2,1,0:T(8,128)S(1)} %dynamic-slice_bitcast_fusion.2, pred[32,128,128]{2,1,0:T(8,128)(4,1)S(1)} %compare_and_fusion.2), kind=kOutput, calls=%fused_computation.1.clone.2 | convolution fusion | flops 268435456 | bytes 2097152 | tf_op jit(solution)/shard_map/while/body/eval_jaxpr/rctj,rcj->rct/dot_general | solution.py:38
  596.8 2.0 copy.55
  598.8 1.5 copy-done.1
  600.3 1.9 slice_reduce_fusion.1
  602.2 1.9 slice_reduce_fusion
  604.8 2.2 multiply_add_fusion
  607.0 3.0 copy.67
  610.0 2.6 reshape.57
  612.6 3.5 fusion.16
  616.1 6.8 copy.57
  622.9 99.6 %all_to_all.18 = f32[2,160,2048]{1,0,2:T(2,128)} all-to-all(f32[2,160,2048]{1,0,2:T(2,128)} %copy.57), channel_id=1, replica_groups=mesh['seq'=16,'chan'=2] {'seq'}, dimensions={2} | all-to-all | bytes 5242880 | tf_op jit(solution)/shard_map/all_to_all | solution.py:85
  722.5 5.3 copy.58
  727.8 4.2 multiply_reduce_fusion
  732.0 5.0 psum.7
  737.0 1.5 fusion.18
  (73 shorter events, 9.7 us)
Async XLA Ops:
  6.6 0.8 copy-start.4
  10.6 1.7 copy-start.2
  598.8 1.5 copy-start.1
  598.8 3.4 copy-start
  727.8 9.2 %copy-start.3 = (f32[2560]{0:T(1024)S(1)}, f32[2560]{0:T(1024)}, u32[]{:S(2)}) copy-start(f32[2560]{0:T(1024)} %param.12) | copy-start | bytes 30724
where the time goes:
time: 742 us; the launch traced here: 739 us
  matrix products  556 us (75%)
  blocking collectives  105 us (14%)
  local copies, waits for them, and re-layouts  42.4 us (6%)
  other arithmetic  20.3 us (3%)
  loops' own time  14.5 us (2%)
    dot_general x5, matrix products, one_group(): jnp.einsum('rctj,rcj->rct', weight, drive_part, precision=lax.Precision.H...  553 us
    all_to_all x1, blocking collectives, per_device(): lax.all_to_all(local_gated, 'seq', split_axis=2, concat_axis=1, tiled=True)  99.6 us

commit v1 on v0

--- a/solution.py
+++ b/solution.py
@@ -1,8 +1,11 @@
+import functools
 import math
 
 import jax
 import jax.numpy as jnp
 from jax import lax
+from jax.experimental import pallas as pl
+from jax.experimental.pallas import tpu as pltpu
 from jax.sharding import PartitionSpec as P
 
 FEATURE_WIDTH = 5120
@@ -86,7 +89,255 @@
     return finish(gated, norm_gain)
 
 
+LANES = 128
+ROWS = 16
+UNROLL = 4
+MESH = pl.DeviceIdType.MESH
+
+
+def scan_blocks(pairs, lane):
+    shift = 1
+    while shift < LANES:
+        inside = lane >= shift
+        advanced = []
+        for decay, drive in pairs:
+            masked = jnp.where(inside, decay, 0.0)
+            drive = drive + masked * pltpu.roll(drive, shift, 1)
+            decay = jnp.where(inside, decay * pltpu.roll(decay, shift, 1), decay)
+            advanced.append((decay, drive))
+        pairs = advanced
+        shift *= 2
+    return pairs
+
+
+def kernel(
+    seq_size, chan_size, resets_ref, step_ref, in_ref, gate_ref, rate_ref, gain_ref, out_ref,
+    step_v, in_v, gate_v, gated, send_v, keep, squares, sums, parts, scales,
+    load_sem, part_send, part_recv, scale_send, scale_recv, data_send, data_recv, own_sem,
+):
+    batch, width, length = step_v.shape
+    blocks = length // LANES
+    devices = seq_size * chan_size
+    my_seq, my_chan = lax.axis_index("seq"), lax.axis_index("chan")
+    mine = my_seq * chan_size + my_chan
+
+    loads = []
+    for b in range(batch):
+        group = []
+        for i, (src, dst) in enumerate(((step_ref, step_v), (in_ref, in_v), (gate_ref, gate_v))):
+            group.append(pltpu.make_async_copy(src.at[b], dst.at[b], load_sem.at[b, i]))
+        for copy in group:
+            copy.start()
+        loads.append(group)
+
+    def peer(d):
+        other = lax.rem(mine + d, devices)
+        return other // chan_size, lax.rem(other, chan_size), other
+
+    barrier = pltpu.get_barrier_semaphore()
+
+    @pl.loop(1, devices)
+    def _(d):
+        ps, pc, _ = peer(d)
+        pl.semaphore_signal(barrier, inc=1, device_id=(ps, pc), device_id_type=MESH)
+
+    lane = lax.broadcasted_iota(jnp.int32, (ROWS, LANES), 1)
+    lane_row = lax.broadcasted_iota(jnp.int32, (8, LANES), 1)
+    zero_rows = jnp.zeros((8, LANES), jnp.float32)
+
+    def prepare(b):
+        @pl.loop(0, blocks)
+        def _(t):
+            place = lane_row + t * LANES
+            hit = place == resets_ref[b, 0]
+            for k in range(1, resets_ref.shape[1]):
+                hit = hit | (place == resets_ref[b, k])
+            keep[t] = jnp.where(hit, 0.0, 1.0)
+            squares[b, t] = zero_rows
+
+    def compute(b, first, last):
+        @pl.loop(first, last)
+        def _(r):
+            rows = pl.ds(pl.multiple_of(r * ROWS, ROWS), ROWS)
+            rate = rate_ref[rows, :]
+
+            def step(sup, carry):
+                pairs, silus = [], []
+                for u in range(UNROLL):
+                    t = sup * UNROLL + u
+                    lanes = pl.ds(pl.multiple_of(t * LANES, LANES), LANES)
+                    x = step_v[b, rows, lanes].astype(jnp.float32) * rate
+                    a = jnp.exp(-x)
+                    y = x + x
+                    series = y * (1.0 - y * (1 / 2 - y * (1 / 6 - y * (1 / 24 - y * (1 / 120 - y * (1 / 720))))))
+                    z = jnp.where(y < 0.25, series, 1.0 - a * a)
+                    root = z * lax.rsqrt(jnp.maximum(z, 1e-37))
+                    drive = root * in_v[b, rows, lanes].astype(jnp.float32)
+                    k8 = keep[t]
+                    decay = a * jnp.concatenate([k8] * (ROWS // 8), axis=0)
+                    pairs.append((decay, drive))
+                pairs = scan_blocks(pairs, lane)
+                for u in range(UNROLL):
+                    t = sup * UNROLL + u
+                    lanes = pl.ds(pl.multiple_of(t * LANES, LANES), LANES)
+                    decay, drive = pairs[u]
+                    state = drive + decay * carry
+                    carry = jnp.broadcast_to(state[:, LANES - 1 :], (ROWS, LANES))
+                    v = gate_v[b, rows, lanes].astype(jnp.float32)
+                    g = state * (v / (1.0 + jnp.exp(-v)))
+                    gated[b, t, rows, :] = g
+                    sq = g * g
+                    part = sq[:8]
+                    for i in range(1, ROWS // 8):
+                        part = part + sq[8 * i : 8 * i + 8]
+                    squares[b, t] += part
+                return carry
+
+            lax.fori_loop(0, blocks // UNROLL, step, jnp.zeros((ROWS, LANES), jnp.float32))
+
+    def send_parts(b):
+        sums[b] = jnp.sum(squares[b], axis=1, keepdims=True)
+        parts[b, mine] = sums[b, my_seq]
+
+        @pl.loop(1, devices)
+        def _(d):
+            ps, pc, _ = peer(d)
+            pltpu.make_async_remote_copy(
+                src_ref=sums.at[b, ps], dst_ref=parts.at[b, mine],
+                send_sem=part_send.at[b, d], recv_sem=part_recv.at[b, mine],
+                device_id=(ps, pc), device_id_type=MESH,
+            ).start()
+
+    def seq_peer(d):
+        return lax.rem(my_seq + d, seq_size)
+
+    def send_scales(b):
+        @pl.loop(1, devices)
+        def _(d):
+            ps, pc, other = peer(d)
+            pltpu.make_async_remote_copy(
+                src_ref=sums.at[b, ps], dst_ref=parts.at[b, other],
+                send_sem=part_send.at[b, d], recv_sem=part_recv.at[b, other],
+                device_id=(ps, pc), device_id_type=MESH,
+            ).wait()
+
+        total = jnp.sum(parts[b], axis=0)
+        scales[b, my_seq] = lax.rsqrt(total / jnp.float32(width * devices) + 1e-05)
+
+        @pl.loop(1, seq_size)
+        def _(d):
+            pltpu.make_async_remote_copy(
+                src_ref=scales.at[b, my_seq], dst_ref=scales.at[b, my_seq],
+                send_sem=scale_send.at[b, d], recv_sem=scale_recv.at[b, my_seq],
+                device_id=(seq_peer(d), my_chan), device_id_type=MESH,
+            ).start()
+
+    my_rows = pl.ds(pl.multiple_of(my_seq * width, width), width)
+
+    def normalize(b, s):
+        send_v[b, s] = (gated[b, s] * scales[b, s] * gain_ref[...]).astype(jnp.bfloat16)
+
+    def data_copy(b, s, d, source):
+        return pltpu.make_async_remote_copy(
+            src_ref=send_v.at[b, s],
+            dst_ref=out_ref.at[b, pl.ds(pl.multiple_of(source * width, width), width), :],
+            send_sem=data_send.at[b, d], recv_sem=data_recv.at[b, source],
+            device_id=(s, my_chan), device_id_type=MESH,
+        )
+
+    def own_copy(b):
+        return pltpu.make_async_copy(send_v.at[b, my_seq], out_ref.at[b, my_rows, :], own_sem.at[b])
+
+    def send_data(b):
+        @pl.loop(1, seq_size)
+        def _(i):
+            d = lax.rem(i + seq_size // 2 - 1, seq_size - 1) + 1
+            s = seq_peer(d)
+            pltpu.make_async_remote_copy(
+                src_ref=scales.at[b, s], dst_ref=scales.at[b, s],
+                send_sem=scale_send.at[b, d], recv_sem=scale_recv.at[b, s],
+                device_id=(s, my_chan), device_id_type=MESH,
+            ).wait()
+            normalize(b, s)
+            data_copy(b, s, d, my_seq).start()
+
+        normalize(b, my_seq)
+        own_copy(b).start()
+
+    def finish_data(b):
+        @pl.loop(1, seq_size)
+        def _(d):
+            s = seq_peer(d)
+            data_copy(b, s, d, s).wait()
+
+        own_copy(b).wait()
+
+    groups = width // ROWS
+    for b in range(batch):
+        for copy in loads[b]:
+            copy.wait()
+        prepare(b)
+        if b == 0:
+            compute(b, 0, groups)
+            pl.semaphore_wait(barrier, devices - 1)
+        else:
+            compute(b, 0, groups // 2)
+            send_scales(b - 1)
+            compute(b, groups // 2, groups)
+        send_parts(b)
+    for b in range(batch - 1):
+        send_data(b)
+    send_scales(batch - 1)
+    send_data(batch - 1)
+    for b in range(batch):
+        finish_data(b)
+
+
+def fused(seq_size, chan_size, step_size, inputs, gate_input, decay_rate, norm_gain, resets):
+    batch, width, length = step_size.shape
+    blocks, devices = length // LANES, seq_size * chan_size
+    start = lax.axis_index("seq") * width
+    rate, gain = (
+        jnp.broadcast_to(lax.dynamic_slice_in_dim(a, start, width)[:, None], (width, LANES))
+        for a in (decay_rate, norm_gain)
+    )
+    f32, dma = jnp.float32, pltpu.SemaphoreType.DMA
+    hbm = pl.BlockSpec(memory_space=pl.ANY)
+    vmem = pl.BlockSpec(memory_space=pltpu.VMEM)
+    return pl.pallas_call(
+        functools.partial(kernel, seq_size, chan_size),
+        out_shape=jax.ShapeDtypeStruct((batch, width * seq_size, LANES), jnp.bfloat16),
+        in_specs=[pl.BlockSpec(memory_space=pltpu.SMEM), hbm, hbm, hbm, vmem, vmem],
+        out_specs=hbm,
+        scratch_shapes=[
+            *(pltpu.VMEM((batch, width, length), jnp.bfloat16) for _ in range(3)),
+            pltpu.VMEM((batch, blocks, width, LANES), f32),
+            pltpu.VMEM((batch, blocks, width, LANES), jnp.bfloat16),
+            pltpu.VMEM((blocks, 8, LANES), f32),
+            pltpu.VMEM((batch, blocks, 8, LANES), f32),
+            pltpu.VMEM((batch, blocks, 1, LANES), f32),
+            pltpu.VMEM((batch, devices, 1, LANES), f32),
+            pltpu.VMEM((batch, blocks, 1, LANES), f32),
+            dma((batch, 3)),
+            dma((batch, devices)), dma((batch, devices)),
+            dma((batch, seq_size)), dma((batch, seq_size)),
+            dma((batch, seq_size)), dma((batch, seq_size)),
+            dma((batch,)),
+        ],
+        compiler_params=pltpu.CompilerParams(collective_id=0, has_side_effects=True),
+    )(resets, step_size, inputs, gate_input, rate, gain)
+
+
 def solution(mesh):
+    seq_size, chan_size = mesh.shape["seq"], mesh.shape["chan"]
+
+    def body(step_size, inputs, gate_input, decay_rate, norm_gain, resets):
+        batch, width, length = step_size.shape
+        fits = width % ROWS == 0 and length == LANES * seq_size
+        if not fits:
+            return per_device(step_size, inputs, gate_input, decay_rate, norm_gain, resets)
+        return fused(seq_size, chan_size, step_size, inputs, gate_input, decay_rate, norm_gain, resets)
+
     in_specs = (
         P(None, ("chan", "seq"), None),
         P(None, ("chan", "seq"), None),
@@ -97,5 +348,5 @@
     )
     out_specs = P(None, "chan", "seq")
     return jax.shard_map(
-        per_device, mesh=mesh, in_specs=in_specs, out_specs=out_specs, check_vma=False
-    )
+        body, mesh=mesh, in_specs=in_specs, out_specs=out_specs, check_vma=False
+    )

time: 742 us -> 113 us (0.15)
  matrix products: 556 us -> 0 us
  Pallas kernels: 0 us -> 108 us
  blocking collectives: 105 us -> 0 us
  local copies, waits for them, and re-layouts: 42.4 us -> 5.43 us
  other arithmetic: 20.3 us -> 0 us
  loops' own time: 14.5 us -> 0 us
    dot_general x7 -> x0, matrix products: 556 us -> none  [the longest x5 553 us: one_group(): jnp.einsum('rctj,rcj->rct', weight, drive_part, precision=lax.Precision.H...]
    pallas_call x0 -> x1, Pallas kernels: none -> 108 us  [fused(): pl.pallas_call(functools.partial(kernel, seq_size, chan_size), out_shape=...]
    all_to_all x1 -> x0, blocking collectives: 99.6 us -> none  [per_device(): lax.all_to_all(local_gated, 'seq', split_axis=2, concat_axis=1, tiled=True)]
    another operation x1 -> x0, loops' own time: 14.5 us -> none  [local_scan(): results = lax.map(one_group, (split_groups(cumul), split_groups(drive)))]
    mul x4 -> x0, other arithmetic: 8.65 us -> none  [the longest x1 5.08 us: coefficients(): drive = jnp.sqrt(-jnp.expm1(-2.0 * scaled)) * values.astype(jnp.float32)]
where the time goes in v1:
time: 113 us
  Pallas kernels  108 us (96%)
  local copies, waits for them, and re-layouts  5.43 us (5%)
    pallas_call x1, Pallas kernels, fused(): pl.pallas_call(functools.partial(kernel, seq_size, chan_size), out_shape=...  108 us
    unnamed x1, local copies, waits for them, and re-layouts  2.46 us

profile of v1, /device:TPU:0, one launch (start us, length us, event | category | flops | bytes accessed | tf_op | source)
XLA Modules:
  0.0 113.1 jit_solution(13404705901823443043)
XLA Ops:
  0.0 0.8 dynamic_slice.6
  0.8 0.8 dynamic_slice.7
  1.5 0.7 broadcast_in_dim.5.gain_ref
  2.3 0.7 broadcast_in_dim.4.rate_ref
  3.0 107.6 %shard_map.64 = bf16[2,2560,128]{2,1,0:T(8,128)(2,1)} custom-call(s32[2,8]{1,0:T(2,128)} %resets_ref.1, bf16[2,160,2048]{2,1,0:T(8,128)(2,1)} %step_ref.1, bf16[2,160,2048]{2,1,0:T(8,128)(2,1)} %in_ref.1, bf16[2,160,2048]{2,1,0:T(8,128)(2,1)} %gate_ref.1, f32[160,128]{1,0:T(8,128)} %broadcast_in_dim.4.rate_ref, f32[160,128]{1,0:T(8,128)} %broadcast_in_dim.5.gain_ref), custom_call_target="tpu_custom_call" | custom-call | tf_op jit(solution)/shard_map/pallas_call | solution.py:307
  110.6 2.5 %copy.8 = bf16[2,2560,128]{2,1,0:T(8,128)(2,1)} copy(bf16[2,2560,128]{2,1,0:T(8,128)(2,1)} %shard_map.64) | data formatting | bytes 2621440

commit v2 on v1

--- a/solution.py
+++ b/solution.py
@@ -90,8 +90,8 @@
 
 
 LANES = 128
-ROWS = 16
-UNROLL = 4
+ROWS = 32
+UNROLL = 16
 MESH = pl.DeviceIdType.MESH
 
 
@@ -177,12 +177,15 @@
                     decay = a * jnp.concatenate([k8] * (ROWS // 8), axis=0)
                     pairs.append((decay, drive))
                 pairs = scan_blocks(pairs, lane)
+                lasts = [
+                    [jnp.broadcast_to(a[:, LANES - 1 :], (ROWS, LANES)) for a in pair] for pair in pairs
+                ]
                 for u in range(UNROLL):
                     t = sup * UNROLL + u
                     lanes = pl.ds(pl.multiple_of(t * LANES, LANES), LANES)
                     decay, drive = pairs[u]
                     state = drive + decay * carry
-                    carry = jnp.broadcast_to(state[:, LANES - 1 :], (ROWS, LANES))
+                    carry = lasts[u][1] + lasts[u][0] * carry
                     v = gate_v[b, rows, lanes].astype(jnp.float32)
                     g = state * (v / (1.0 + jnp.exp(-v)))
                     gated[b, t, rows, :] = g

time: 113 us -> 60.2 us (0.53)
  Pallas kernels: 108 us -> 54.2 us
    pallas_call x1, Pallas kernels: 108 us -> 54.2 us  [fused(): pl.pallas_call(functools.partial(kernel, seq_size, chan_size), out_shape=...]
where the time goes in v2:
time: 60.2 us; the launch traced here: 59.7 us
  Pallas kernels  54.2 us (90%)
  local copies, waits for them, and re-layouts  5.43 us (9%)
    pallas_call x1, Pallas kernels, fused(): pl.pallas_call(functools.partial(kernel, seq_size, chan_size), out_shape=...  54.2 us
    unnamed x1, local copies, waits for them, and re-layouts  2.46 us
    dynamic_slice x2, local copies, waits for them, and re-layouts, fused(): lax.dynamic_slice_in_dim(a, start, width)[:, None]  1.54 us
    broadcast_in_dim x2, local copies, waits for them, and re-layouts, fused(): jnp.broadcast_to(lax.dynamic_slice_in_dim(a, start, width)[:, None], (wid...  1.44 us

profile of v2, /device:TPU:0, one launch (start us, length us, event | category | flops | bytes accessed | tf_op | source)
XLA Modules:
  0.0 59.7 jit_solution(4088204335318627052)
XLA Ops:
  0.0 0.8 %dynamic_slice.6 = f32[160]{0:T(256)S(1)} dynamic-slice(f32[2560]{0:T(1024)} %param.9, s32[]{:T(128)S(6)} %select_n.4), dynamic_slice_sizes={160} | dynamic-slice | bytes 1284 | tf_op jit(solution)/shard_map/dynamic_slice | solution.py:304
  0.8 0.8 %dynamic_slice.7 = f32[160]{0:T(256)S(1)} dynamic-slice(f32[2560]{0:T(1024)} %param.10, s32[]{:T(128)S(6)} %select_n.4), dynamic_slice_sizes={160} | dynamic-slice | bytes 1284 | tf_op jit(solution)/shard_map/dynamic_slice | solution.py:304
  1.5 0.7 %broadcast_in_dim.5.gain_ref = f32[160,128]{1,0:T(8,128)} broadcast(f32[160]{0:T(256)S(1)} %dynamic_slice.7), dimensions={0} | broadcast | bytes 82560 | tf_op jit(solution)/shard_map/broadcast_in_dim | solution.py:304
  2.3 0.7 %broadcast_in_dim.4.rate_ref = f32[160,128]{1,0:T(8,128)} broadcast(f32[160]{0:T(256)S(1)} %dynamic_slice.6), dimensions={0} | broadcast | bytes 82560 | tf_op jit(solution)/shard_map/broadcast_in_dim | solution.py:304
  3.0 54.2 %shard_map.64 = bf16[2,2560,128]{2,1,0:T(8,128)(2,1)} custom-call(s32[2,8]{1,0:T(2,128)} %resets_ref.1, bf16[2,160,2048]{2,1,0:T(8,128)(2,1)} %step_ref.1, bf16[2,160,2048]{2,1,0:T(8,128)(2,1)} %in_ref.1, bf16[2,160,2048]{2,1,0:T(8,128)(2,1)} %gate_ref.1, f32[160,128]{1,0:T(8,128)} %broadcast_in_dim.4.rate_ref, f32[160,128]{1,0:T(8,128)} %broadcast_in_dim.5.gain_ref), custom_call_target="tpu_custom_call" | custom-call | tf_op jit(solution)/shard_map/pallas_call | solution.py:310
  57.2 2.5 %copy.8 = bf16[2,2560,128]{2,1,0:T(8,128)(2,1)} copy(bf16[2,2560,128]{2,1,0:T(8,128)(2,1)} %shard_map.64) | data formatting | bytes 2621440

commit v3 on v2

--- a/solution.py
+++ b/solution.py
@@ -91,6 +91,7 @@
 
 LANES = 128
 ROWS = 32
+INNER = 4
 UNROLL = 16
 MESH = pl.DeviceIdType.MESH
 
@@ -112,15 +113,24 @@
 
 def kernel(
     seq_size, chan_size, resets_ref, step_ref, in_ref, gate_ref, rate_ref, gain_ref, out_ref,
-    step_v, in_v, gate_v, gated, send_v, keep, squares, sums, parts, scales,
-    load_sem, part_send, part_recv, scale_send, scale_recv, data_send, data_recv, own_sem,
+    step_v, in_v, gate_v, small_v, columns, gated, send_v, keep, squares, near, far, scales,
+    load_sem, small_sem, near_send, near_recv, far_send, far_recv, data_send, data_recv, own_sem,
 ):
     batch, width, length = step_v.shape
     blocks = length // LANES
     devices = seq_size * chan_size
     my_seq, my_chan = lax.axis_index("seq"), lax.axis_index("chan")
     mine = my_seq * chan_size + my_chan
-
+    inner = math.gcd(seq_size, INNER)
+    outer = seq_size // inner
+    plane = inner * chan_size
+    my_place, my_outer = lax.rem(mine, plane), mine // plane
+
+    smalls = [
+        pltpu.make_async_copy(src, small_v.at[i], small_sem.at[i]) for i, src in enumerate((rate_ref, gain_ref))
+    ]
+    for copy in smalls:
+        copy.start()
     loads = []
     for b in range(batch):
         group = []
@@ -150,16 +160,28 @@
         def _(t):
             place = lane_row + t * LANES
             hit = place == resets_ref[b, 0]
-            for k in range(1, resets_ref.shape[1]):
-                hit = hit | (place == resets_ref[b, k])
-            keep[t] = jnp.where(hit, 0.0, 1.0)
+            for n in range(1, resets_ref.shape[1]):
+                hit = hit | (place == resets_ref[b, n])
+            keep[b, t] = jnp.where(hit, 0.0, 1.0)
             squares[b, t] = zero_rows
+
+    first_channel = my_seq * width
+    channel_row, channel_shift = first_channel // LANES, lax.rem(first_channel, LANES)
+
+    def make_columns():
+        for i in range(2):
+            for n in range(columns.shape[1] // LANES):
+                row = small_v[i, pl.ds(jnp.minimum(channel_row + n, small_v.shape[1] - 1), 1), :]
+                columns[i, n * LANES : (n + 1) * LANES, :] = jnp.transpose(jnp.broadcast_to(row, (LANES, LANES)))
+
+    def column(i, start, size):
+        return columns[i, pl.ds(pl.multiple_of(channel_shift + start, math.gcd(width, LANES)), size), :]
 
     def compute(b, first, last):
         @pl.loop(first, last)
         def _(r):
             rows = pl.ds(pl.multiple_of(r * ROWS, ROWS), ROWS)
-            rate = rate_ref[rows, :]
+            rate = column(0, r * ROWS, ROWS)
 
             def step(sup, carry):
                 pairs, silus = [], []
@@ -173,7 +195,7 @@
                     z = jnp.where(y < 0.25, series, 1.0 - a * a)
                     root = z * lax.rsqrt(jnp.maximum(z, 1e-37))
                     drive = root * in_v[b, rows, lanes].astype(jnp.float32)
-                    k8 = keep[t]
+                    k8 = keep[b, t]
                     decay = a * jnp.concatenate([k8] * (ROWS // 8), axis=0)
                     pairs.append((decay, drive))
                 pairs = scan_blocks(pairs, lane)
@@ -198,47 +220,55 @@
 
             lax.fori_loop(0, blocks // UNROLL, step, jnp.zeros((ROWS, LANES), jnp.float32))
 
-    def send_parts(b):
-        sums[b] = jnp.sum(squares[b], axis=1, keepdims=True)
-        parts[b, mine] = sums[b, my_seq]
-
-        @pl.loop(1, devices)
-        def _(d):
-            ps, pc, _ = peer(d)
-            pltpu.make_async_remote_copy(
-                src_ref=sums.at[b, ps], dst_ref=parts.at[b, mine],
-                send_sem=part_send.at[b, d], recv_sem=part_recv.at[b, mine],
-                device_id=(ps, pc), device_id_type=MESH,
-            ).start()
+    def near_copy(b, d, source):
+        place = lax.rem(my_place + d, plane)
+        return pltpu.make_async_remote_copy(
+            src_ref=near.at[b, my_place], dst_ref=near.at[b, source],
+            send_sem=near_send.at[b, d], recv_sem=near_recv.at[b, source],
+            device_id=(my_outer * inner + place // chan_size, lax.rem(place, chan_size)), device_id_type=MESH,
+        )
+
+    def far_copy(b, d, source):
+        place = lax.rem(my_outer + d, outer)
+        return pltpu.make_async_remote_copy(
+            src_ref=far.at[b, my_outer], dst_ref=far.at[b, source],
+            send_sem=far_send.at[b, d], recv_sem=far_recv.at[b, source],
+            device_id=(place * inner + lax.rem(my_seq, inner), my_chan), device_id_type=MESH,
+        )
+
+    def send_near(b):
+        near[b, my_place] = jnp.sum(squares[b], axis=1)
+
+        @pl.loop(1, plane)
+        def _(d):
+            near_copy(b, d, my_place).start()
+
+    def send_far(b):
+        @pl.loop(1, plane)
+        def _(d):
+            near_copy(b, d, lax.rem(my_place + d, plane)).wait()
+
+        far[b, my_outer] = jnp.sum(near[b], axis=0)
+
+        @pl.loop(1, outer)
+        def _(d):
+            far_copy(b, d, my_outer).start()
+
+    def make_scales(b):
+        @pl.loop(1, outer)
+        def _(d):
+            far_copy(b, d, lax.rem(my_outer + d, outer)).wait()
+
+        total = jnp.sum(far[b], axis=0)
+        scales[b] = lax.rsqrt(total / jnp.float32(width * devices) + 1e-05)
 
     def seq_peer(d):
         return lax.rem(my_seq + d, seq_size)
 
-    def send_scales(b):
-        @pl.loop(1, devices)
-        def _(d):
-            ps, pc, other = peer(d)
-            pltpu.make_async_remote_copy(
-                src_ref=sums.at[b, ps], dst_ref=parts.at[b, other],
-                send_sem=part_send.at[b, d], recv_sem=part_recv.at[b, other],
-                device_id=(ps, pc), device_id_type=MESH,
-            ).wait()
-
-        total = jnp.sum(parts[b], axis=0)
-        scales[b, my_seq] = lax.rsqrt(total / jnp.float32(width * devices) + 1e-05)
-
-        @pl.loop(1, seq_size)
-        def _(d):
-            pltpu.make_async_remote_copy(
-                src_ref=scales.at[b, my_seq], dst_ref=scales.at[b, my_seq],
-                send_sem=scale_send.at[b, d], recv_sem=scale_recv.at[b, my_seq],
-                device_id=(seq_peer(d), my_chan), device_id_type=MESH,
-            ).start()
-
     my_rows = pl.ds(pl.multiple_of(my_seq * width, width), width)
 
     def normalize(b, s):
-        send_v[b, s] = (gated[b, s] * scales[b, s] * gain_ref[...]).astype(jnp.bfloat16)
+        send_v[b, s] = (gated[b, s] * scales[b, pl.ds(s, 1), :] * column(1, 0, width)).astype(jnp.bfloat16)
 
     def data_copy(b, s, d, source):
         return pltpu.make_async_remote_copy(
@@ -253,14 +283,8 @@
 
     def send_data(b):
         @pl.loop(1, seq_size)
-        def _(i):
-            d = lax.rem(i + seq_size // 2 - 1, seq_size - 1) + 1
+        def _(d):
             s = seq_peer(d)
-            pltpu.make_async_remote_copy(
-                src_ref=scales.at[b, s], dst_ref=scales.at[b, s],
-                send_sem=scale_send.at[b, d], recv_sem=scale_recv.at[b, s],
-                device_id=(s, my_chan), device_id_type=MESH,
-            ).wait()
             normalize(b, s)
             data_copy(b, s, d, my_seq).start()
 
@@ -276,21 +300,28 @@
         own_copy(b).wait()
 
     groups = width // ROWS
+    for b in range(batch):
+        prepare(b)
+    for copy in smalls:
+        copy.wait()
+    make_columns()
     for b in range(batch):
         for copy in loads[b]:
             copy.wait()
-        prepare(b)
         if b == 0:
             compute(b, 0, groups)
             pl.semaphore_wait(barrier, devices - 1)
         else:
-            compute(b, 0, groups // 2)
-            send_scales(b - 1)
-            compute(b, groups // 2, groups)
-        send_parts(b)
+            split = groups * 3 // 5
+            compute(b, 0, split)
+            send_far(b - 1)
+            compute(b, split, groups)
+        send_near(b)
     for b in range(batch - 1):
+        make_scales(b)
         send_data(b)
-    send_scales(batch - 1)
+    send_far(batch - 1)
+    make_scales(batch - 1)
     send_data(batch - 1)
     for b in range(batch):
         finish_data(b)
@@ -299,31 +330,32 @@
 def fused(seq_size, chan_size, step_size, inputs, gate_input, decay_rate, norm_gain, resets):
     batch, width, length = step_size.shape
     blocks, devices = length // LANES, seq_size * chan_size
-    start = lax.axis_index("seq") * width
-    rate, gain = (
-        jnp.broadcast_to(lax.dynamic_slice_in_dim(a, start, width)[:, None], (width, LANES))
-        for a in (decay_rate, norm_gain)
-    )
+    inner = math.gcd(seq_size, INNER)
+    outer, plane = seq_size // inner, inner * chan_size
+    rate, gain = decay_rate.reshape(-1, LANES), norm_gain.reshape(-1, LANES)
+    span = LANES - math.gcd(width, LANES) + width
+    column_rows = -(-span // LANES) * LANES
     f32, dma = jnp.float32, pltpu.SemaphoreType.DMA
     hbm = pl.BlockSpec(memory_space=pl.ANY)
-    vmem = pl.BlockSpec(memory_space=pltpu.VMEM)
     return pl.pallas_call(
         functools.partial(kernel, seq_size, chan_size),
         out_shape=jax.ShapeDtypeStruct((batch, width * seq_size, LANES), jnp.bfloat16),
-        in_specs=[pl.BlockSpec(memory_space=pltpu.SMEM), hbm, hbm, hbm, vmem, vmem],
+        in_specs=[pl.BlockSpec(memory_space=pltpu.SMEM), hbm, hbm, hbm, hbm, hbm],
         out_specs=hbm,
         scratch_shapes=[
             *(pltpu.VMEM((batch, width, length), jnp.bfloat16) for _ in range(3)),
+            pltpu.VMEM((2, *rate.shape), f32),
+            pltpu.VMEM((2, column_rows, LANES), f32),
             pltpu.VMEM((batch, blocks, width, LANES), f32),
             pltpu.VMEM((batch, blocks, width, LANES), jnp.bfloat16),
-            pltpu.VMEM((blocks, 8, LANES), f32),
             pltpu.VMEM((batch, blocks, 8, LANES), f32),
-            pltpu.VMEM((batch, blocks, 1, LANES), f32),
-            pltpu.VMEM((batch, devices, 1, LANES), f32),
-            pltpu.VMEM((batch, blocks, 1, LANES), f32),
-            dma((batch, 3)),
-            dma((batch, devices)), dma((batch, devices)),
-            dma((batch, seq_size)), dma((batch, seq_size)),
+            pltpu.VMEM((batch, blocks, 8, LANES), f32),
+            pltpu.VMEM((batch, plane, blocks, LANES), f32),
+            pltpu.VMEM((batch, outer, blocks, LANES), f32),
+            pltpu.VMEM((batch, blocks, LANES), f32),
+            dma((batch, 3)), dma((2,)),
+            dma((batch, plane)), dma((batch, plane)),
+            dma((batch, outer)), dma((batch, outer)),
             dma((batch, seq_size)), dma((batch, seq_size)),
             dma((batch,)),
         ],
@@ -337,6 +369,7 @@
     def body(step_size, inputs, gate_input, decay_rate, norm_gain, resets):
         batch, width, length = step_size.shape
         fits = width % ROWS == 0 and length == LANES * seq_size
+        fits = fits and (width * seq_size) % LANES == 0
         if not fits:
             return per_device(step_size, inputs, gate_input, decay_rate, norm_gain, resets)
         return fused(seq_size, chan_size, step_size, inputs, gate_input, decay_rate, norm_gain, resets)

time: 60.2 us -> 51.5 us (0.86)
  the two profiles are of different devices: /device:TPU:0 before, /device:TPU:11 now
where the time goes in v3:
time: 51.5 us; the launch traced here: 51.3 us
  Pallas kernels  48.8 us (95%)
  local copies, waits for them, and re-layouts  2.46 us (5%)
    pallas_call x1, Pallas kernels, fused(): pl.pallas_call(functools.partial(kernel, seq_size, chan_size), out_shape=...  48.8 us
    unnamed x1, local copies, waits for them, and re-layouts  2.46 us

profile of v3, /device:TPU:11, one launch (start us, length us, event | category | flops | bytes accessed | tf_op | source)
XLA Modules:
  0.0 51.3 jit_solution(17954003675223645705)
XLA Ops:
  0.0 48.8 %shard_map.64 = bf16[2,2560,128]{2,1,0:T(8,128)(2,1)} custom-call(s32[2,8]{1,0:T(2,128)} %resets_ref.1, bf16[2,160,2048]{2,1,0:T(8,128)(2,1)} %step_ref.1, bf16[2,160,2048]{2,1,0:T(8,128)(2,1)} %in_ref.1, bf16[2,160,2048]{2,1,0:T(8,128)(2,1)} %gate_ref.1, f32[20,128]{1,0:T(8,128)} %bitcast.2, f32[20,128]{1,0:T(8,128)} %bitcast.3), custom_call_target="tpu_custom_call" | custom-call | tf_op jit(solution)/shard_map/pallas_call | solution.py:340
  48.8 2.5 %copy.8 = bf16[2,2560,128]{2,1,0:T(8,128)(2,1)} copy(bf16[2,2560,128]{2,1,0:T(8,128)(2,1)} %shard_map.64) | data formatting | bytes 2621440
